TPU v7x, 32 devices: a whole 2x2x4 slice. The times are simulated.
32 devices in a mesh: rows: 8 (over y, x, core), feat: 4 (over z).
Axes of the slice: x: 2, y: 2, z: 4, core: 2. Of those that a mesh axis runs over, the one named last changes fastest.
Arguments:
- features: bfloat16 [8192, 2048], P('rows', 'feat'), may hold values from -6 to 6
- grad_out: bfloat16 [8192, 2048], P('rows', 'feat'), may hold values from -6 to 6
- eigvecs: float32 [2048, 2048], P('feat', 'rows'), may hold values from -1 to 1, as said below
- eigvals: float32 [2048], replicated, may hold values from 0.1 to 1, as said below
- whiten: bfloat16 [2048, 2048], P(None, 'feat'), may hold values from -0.125 to 0.125
Outputs:
- grad_in: bfloat16 [8192, 2048], P('rows', 'feat')
Inputs may be any that keep to these rules, and one draw needn't show every extreme that they name: `eigvecs`: the columns are orthonormal. `eigvals`: any two entries differ by at least 0.45 / 2048.
All inputs are finite; a program needn't handle non-finite values.
Results may differ from a plain program's by a relative error of at most 0.0074.
Values may be sent and summed in bfloat16 or wider, within the bound.
A program may use at most 128 MiB of HBM per device.

v0:
```python
import jax
import jax.numpy as jnp
from jax import lax
from jax.sharding import PartitionSpec as P


def divided(lam_row, lam_col, first_col):
    on_diag = (
        jnp.arange(lam_row.shape[0], dtype=jnp.int32)[:, None]
        == (first_col + jnp.arange(lam_col.shape[0], dtype=jnp.int32))[None, :]
    )
    root_row = lam_row ** (-0.5)
    root_col = lam_col ** (-0.5)
    gaps_lam = lam_row[:, None] - lam_col[None, :]
    safe_gap = jnp.where(on_diag, jnp.ones_like(gaps_lam), gaps_lam)
    off_diag = (root_row[:, None] - root_col[None, :]) / safe_gap
    diag_vals = -0.5 * lam_row[:, None] ** (-1.5) + jnp.zeros_like(gaps_lam)
    return jnp.where(on_diag, diag_vals, off_diag)


def local(features, grad_out, eigvecs, eigvals, whiten):
    highest = lax.Precision.HIGHEST
    tok_rows, own_cols = features.shape
    row_count = tok_rows * lax.axis_size("rows")
    contract_rows = (((0,), (0,)), ((), ()))
    contract_last = (((1,), (1,)), ((), ()))
    piece_x = lax.all_gather(features, "feat", axis=1, tiled=True)
    piece_g = lax.all_gather(grad_out, "feat", axis=1, tiled=True)
    left_part = lax.dot_general(
        features, piece_g, contract_rows, preferred_element_type=jnp.float32
    )
    right_part = lax.dot_general(
        grad_out, piece_x, contract_rows, preferred_element_type=jnp.float32
    )
    cross_one = left_part
    cross_two = right_part
    sum_x = jnp.sum(piece_x, axis=0, dtype=jnp.float32)
    sum_g = jnp.sum(piece_g, axis=0, dtype=jnp.float32)
    cross_one, cross_two, sum_x, sum_g = (cross_one, cross_two, sum_x, sum_g)
    cross_one, cross_two, sum_x, sum_g = lax.psum((cross_one, cross_two, sum_x, sum_g), "rows")
    both_cross = cross_one + cross_two
    col_mean = sum_x / row_count
    grad_mean = sum_g / row_count
    offset = lax.axis_index("feat") * own_cols
    mean_part = lax.dynamic_slice_in_dim(col_mean, offset, own_cols)
    grad_part = lax.dynamic_slice_in_dim(grad_mean, offset, own_cols)
    sym_gram = 0.5 * (
        both_cross
        - row_count
        * (mean_part[:, None] * grad_mean[None, :] + grad_part[:, None] * col_mean[None, :])
    )
    basis_cols = lax.all_gather(eigvecs, "feat", axis=0, tiled=True)
    basis_block = lax.all_gather(eigvecs, "rows", axis=1, tiled=True)
    narrow = basis_cols.shape[1]
    inner_prod = jnp.dot(sym_gram, basis_cols, precision=highest)
    partial_value = lax.dot_general(basis_block, inner_prod, contract_rows, precision=highest)
    rotated = lax.psum(partial_value, "feat")
    first_col = lax.axis_index("rows") * narrow
    lam_col = lax.dynamic_slice_in_dim(eigvals, first_col, narrow)
    scaled = divided(eigvals, lam_col, first_col) * rotated
    back_rot = jnp.dot(basis_block, scaled, precision=highest)
    sens_own = lax.psum_scatter(
        lax.dot_general(back_rot, basis_cols, contract_last, precision=highest),
        "rows",
        scatter_dimension=0,
        tiled=True,
    )
    scaled_own = (2.0 / row_count * sens_own).astype(jnp.bfloat16)
    sens_scaled = lax.all_gather(scaled_own, "rows", axis=0, tiled=True)
    piece_x = lax.all_gather(features, "feat", axis=1, tiled=True)
    piece_g = lax.all_gather(grad_out, "feat", axis=1, tiled=True)
    shifted = (piece_g.astype(jnp.float32) - grad_mean).astype(jnp.bfloat16)
    centered = (piece_x.astype(jnp.float32) - col_mean).astype(jnp.bfloat16)
    running = jnp.dot(shifted, whiten, preferred_element_type=jnp.float32)
    grad_in = running + lax.dot_general(
        centered, sens_scaled, contract_last, preferred_element_type=jnp.float32
    )
    return grad_in.astype(jnp.bfloat16)


def solution(mesh):
    in_specs = (P("rows", "feat"), P("rows", "feat"), P("feat", "rows"), P(), P(None, "feat"))
    out_specs = P("rows", "feat")
    return jax.shard_map(local, mesh=mesh, in_specs=in_specs, out_specs=out_specs, check_vma=False)
```

profile of v0, /device:TPU:0, one launch (start us, length us, event | category | flops | bytes accessed | tf_op | source)
XLA Modules:
  0.0 552.3 jit_solution(13871746332786428748)
XLA Ops:
  6.5 0.7 all-gather.6.cloned.1.call-update
  7.3 0.7 all-gather.8.cloned.1.call-update
  8.1 0.7 all-gather.10.cloned.1.call-update
  8.8 83.6 %all-gather.6.cloned.1.call-done = bf16[1024,2048]{1,0:T(8,128)(2,1)} async-done(((bf16[1024,512]{1,0:T(8,128)(2,1)}), bf16[1024,2048]{1,0:T(8,128)(2,1)}) %all-gather.6.cloned.1.call-update) | async-done | bytes 4194320 | tf_op jit(solution)/shard_map/all_gather | solution.py:71
  92.4 6.8 %fusion.40 = f32[512,2048]{1,0:T(8,128)} fusion(bf16[1024,512]{1,0:T(8,128)(2,1)} %param.5, bf16[1024,2048]{1,0:T(8,128)(2,1)} %all-gather.6.cloned.1.call-done), kind=kOutput, calls=%fused_computation.51 | convolution fusion | flops 2147483648 | bytes 9437184 | tf_op jit(solution)/shard_map/dot_general | solution.py:29
  99.2 74.0 %all-gather.8.cloned.1.call-done = bf16[1024,2048]{1,0:T(8,128)(2,1)} async-done(((bf16[1024,512]{1,0:T(8,128)(2,1)}), bf16[1024,2048]{1,0:T(8,128)(2,1)}) %all-gather.8.cloned.1.call-update) | async-done | bytes 4194320 | tf_op jit(solution)/shard_map/all_gather | solution.py:70
  173.2 7.8 %convolution_add_fusion = f32[512,2048]{1,0:T(8,128)} fusion(f32[512,2048]{1,0:T(8,128)} %fusion.40, bf16[1024,512]{1,0:T(8,128)(2,1)S(1)} %copy-done.3, bf16[1024,2048]{1,0:T(8,128)(2,1)} %all-gather.8.cloned.1.call-done), kind=kOutput, calls=%fused_computation.17 | convolution fusion | flops 2148532224 | bytes 13631488 | tf_op jit(solution)/shard_map/dot_general | solution.py:32
  181.1 0.0 all-gather.12.cloned.1.call-start
  181.1 0.5 all-gather.12.cloned.1.call-update
  181.7 0.0 all-reduce.4.cloned.1.call-start
  181.7 3.0 convert_reduce_fusion
  184.7 0.5 copy-done.1
  185.2 0.6 convert_reduce_fusion.1
  185.8 25.6 %all-reduce = (f32[2048]{0:T(1024)S(1)}, f32[2048]{0:T(1024)S(1)}) all-reduce(f32[2048]{0:T(1024)S(1)} %convert_reduce_fusion, f32[2048]{0:T(1024)S(1)} %convert_reduce_fusion.1), channel_id=1, replica_groups=mesh['rows'=8,'feat'=4] {'rows'}, use_global_device_ids=true, to_apply=%region_3.0 | all-reduce | flops 4096 | bytes 32768 | tf_op jit(solution)/shard_map/psum | solution.py:40
  211.4 0.1 dynamic_slice.10
  211.5 0.1 dynamic_slice.11
  211.6 7.4 %all-gather.10.cloned.1.call-done = f32[2048,256]{1,0:T(8,128)} async-done(((f32[512,256]{1,0:T(8,128)}), f32[2048,256]{1,0:T(8,128)}) %all-gather.10.cloned.1.call-update) | async-done | bytes 2097168 | tf_op jit(solution)/shard_map/all_gather | solution.py:52
  219.0 82.8 %all-reduce.6.cloned.1.call-done = f32[512,2048]{1,0:T(8,128)} async-done(((f32[512,2048]{1,0:T(8,128)}), f32[512,2048]{1,0:T(8,128)}) %all-reduce.6.cloned.1.call-update) | async-done | bytes 4194320 | tf_op jit(solution)/shard_map/psum | solution.py:40
  301.7 6.9 %fusion.6 = f32[512,256]{1,0:T(8,128)S(1)} fusion(f32[2048,256]{1,0:T(8,128)} %all-gather.10.cloned.1.call-done, f32[512,2048]{1,0:T(8,128)} %all-reduce.6.cloned.1.call-done, f32[2048]{0:T(1024)S(1)} %get-tuple-element.11, f32[512]{0:T(512)S(1)} %dynamic_slice.11, f32[2048]{0:T(1024)S(1)} %get-tuple-element.12, f32[512]{0:T(512)S(1)} %dynamic_slice.10), kind=kOutput, calls=%fused_computation.8 | convolution fusion | flops 3227516928 | bytes 6836224 | tf_op jit(solution)/shard_map/dot_general | solution.py:55
  308.6 32.3 %all-gather.12.cloned.1.call-done = f32[512,2048]{1,0:T(8,128)} async-done(((f32[512,256]{1,0:T(8,128)}), f32[512,2048]{1,0:T(8,128)}) %all-gather.12.cloned.1.call-update) | async-done | bytes 4194320 | tf_op jit(solution)/shard_map/all_gather | solution.py:53
  340.9 10.2 %convolution_bitcast_fusion = f32[2048,256]{1,0:T(8,128)} fusion(f32[512,256]{1,0:T(8,128)S(1)} %fusion.6, f32[512,2048]{1,0:T(8,128)} %all-gather.12.cloned.1.call-done), kind=kOutput, calls=%fused_computation.18 | convolution fusion | flops 3221225472 | bytes 6815744 | tf_op jit(solution)/shard_map/dot_general | solution.py:56
  351.1 0.3 reduce-scatter.2.cloned.1.call-start
  351.4 0.1 broadcast_power_fusion.1
  351.5 85.9 %all-reduce.4.cloned.1.call-done = f32[2048,256]{1,0:T(8,128)} async-done(((f32[2048,256]{1,0:T(8,128)}), f32[2048,256]{1,0:T(8,128)}) %all-reduce.4.cloned.1.call-update) | async-done | bytes 2097168 | tf_op jit(solution)/shard_map/psum | solution.py:57
  437.4 10.8 %fusion.15 = f32[256,512]{1,0:T(8,128)S(1)} fusion(f32[512,2048]{1,0:T(8,128)} %all-gather.12.cloned.1.call-done, f32[2048,256]{1,0:T(8,128)} %all-reduce.4.cloned.1.call-done, f32[256]{0:T(256)S(1)} %get-tuple-element.8, f32[2048]{0:T(1024)S(1)} %copy-done.5, f32[256]{0:T(256)S(1)} %get-tuple-element.7, f32[2048]{0:T(1024)S(1)} %get-tuple-element.10, ...), kind=kOutput, calls=%fused_computation.20 | convolution fusion | flops 3224895488 | bytes 6843392 | tf_op jit(solution)/shard_map/dot_general | solution.py:61
  448.2 8.4 %fusion.41 = f32[512,2048]{1,0:T(8,128)} fusion(f32[256,512]{1,0:T(8,128)S(1)} %fusion.15, f32[2048,256]{1,0:T(8,128)S(1)} %copy-done.4), kind=kOutput, calls=%fused_computation.52 | convolution fusion | flops 3221225472 | bytes 6815744 | tf_op jit(solution)/shard_map/dot_general | solution.py:63
  456.7 0.3 all-gather.14.cloned.1.call-start
  457.0 50.0 %reduce-scatter.2.cloned.1.call-done = f32[64,2048]{1,0:T(8,128)} async-done(((f32[512,2048]{1,0:T(8,128)}), f32[64,2048]{1,0:T(8,128)}) %reduce-scatter.2.cloned.1.call-update) | async-done | bytes 524304 | tf_op jit(solution)/shard_map/reduce_scatter | solution.py:62
  507.0 1.8 multiply_convert_fusion
  508.8 27.9 %all-gather.14.cloned.1.call-done = bf16[512,2048]{1,0:T(8,128)(2,1)} async-done(((bf16[64,2048]{1,0:T(8,128)(2,1)}), bf16[512,2048]{1,0:T(8,128)(2,1)}) %all-gather.14.cloned.1.call-update) | async-done | bytes 2097168 | tf_op jit(solution)/shard_map/all_gather | solution.py:69
  536.7 5.4 fusion.2
  542.1 3.3 add_convert_fusion
  (22 shorter events, 0.2 us)
Async XLA Ops:
  6.5 535.6 %copy-start = (bf16[2048,512]{1,0:T(8,128)(2,1)S(1)}, bf16[2048,512]{1,0:T(8,128)(2,1)}, u32[]{:S(2)}) copy-start(bf16[2048,512]{1,0:T(8,128)(2,1)} %param.9) | copy-start | bytes 6291460
  6.5 85.9 %all-gather.6.cloned.1.call-start = ((), (), s32[]{:S(2)}) async-start(), calls=%async_computation.1 | async-start | bytes 5242880 | tf_op jit(solution)/shard_map/all_gather | solution.py:71
  7.3 166.0 %all-gather.8.cloned.1.call-start = ((), (), s32[]{:S(2)}) async-start(), calls=%async_computation.2 | async-start | bytes 5242880 | tf_op jit(solution)/shard_map/all_gather | solution.py:70
  8.0 211.0 %all-gather.10.cloned.1.call-start = ((), (), s32[]{:S(2)}) async-start(), calls=%async_computation.3 | async-start | bytes 2621440 | tf_op jit(solution)/shard_map/all_gather | solution.py:52
  8.7 164.5 %copy-start.3 = (bf16[1024,512]{1,0:T(8,128)(2,1)S(1)}, bf16[1024,512]{1,0:T(8,128)(2,1)}, u32[]{:S(2)}) copy-start(bf16[1024,512]{1,0:T(8,128)(2,1)} %param.6) | copy-start | bytes 3145732
  8.8 293.0 %all-reduce.6.cloned.1.call-start = ((), (), s32[]{:S(2)}) async-start(), calls=%async_computation.8 | async-start | bytes 8388608 | tf_op jit(solution)/shard_map/psum | solution.py:40
  181.1 159.9 %all-gather.12.cloned.1.call-start = ((), (), s32[]{:S(2)}) async-start(), calls=%async_computation.4 | async-start | bytes 4718592 | tf_op jit(solution)/shard_map/all_gather | solution.py:53
  181.7 255.8 %all-reduce.4.cloned.1.call-start = ((), (), s32[]{:S(2)}) async-start(), calls=%async_computation.5 | async-start | bytes 4194304 | tf_op jit(solution)/shard_map/psum | solution.py:57
  181.7 3.5 copy-start.1
  308.6 42.8 %copy-start.5 = (f32[2048]{0:T(1024)S(1)}, f32[2048]{0:T(1024)}, u32[]{:S(2)}) copy-start(f32[2048]{0:T(1024)} %param.8) | copy-start | bytes 24580
  351.1 155.9 %reduce-scatter.2.cloned.1.call-start = ((), (), s32[]{:S(2)}) async-start(), calls=%async_computation.6 | async-start | bytes 4718592 | tf_op jit(solution)/shard_map/reduce_scatter | solution.py:62
  437.4 10.8 %copy-start.4 = (f32[2048,256]{1,0:T(8,128)S(1)}, f32[2048,256]{1,0:T(8,128)}, u32[]{:S(2)}) copy-start(f32[2048,256]{1,0:T(8,128)} %all-gather.10.cloned.1.call-done) | copy-start | bytes 6291460
  456.7 80.1 %all-gather.14.cloned.1.call-start = ((), (), s32[]{:S(2)}) async-start(), calls=%async_computation.7 | async-start | bytes 2359296 | tf_op jit(solution)/shard_map/all_gather | solution.py:69
  536.7 5.4 copy-start.2
Sparse Core Ops, SparseCore 0:
  8.9 83.4 all-gather.5
  94.0 79.2 all-gather.7
  174.8 44.1 all-gather.9
  222.1 79.5 all-reduce.5
  303.5 37.3 all-gather.11
  351.3 86.1 all-reduce.3
  456.8 50.1 reduce-scatter.1
  508.9 27.7 all-gather.13
where the time goes:
time: 552 us
  waiting for transfers between devices  447 us (81%)
  matrix products  59.6 us (11%)
  blocking collectives  25.6 us (5%)
  between operations  13.6 us (2%)
    psum x1, waiting for transfers between devices, local(): rotated = lax.psum(partial_value, 'feat')  85.9 us
    all_gather x1, waiting for transfers between devices, local(): piece_g = lax.all_gather(grad_out, 'feat', axis=1, tiled=True)  83.6 us
    psum x1, waiting for transfers between devices, local(): lax.psum((cross_one, cross_two, sum_x, sum_g), 'rows')  82.8 us
    all_gather x1, waiting for transfers between devices, local(): piece_x = lax.all_gather(features, 'feat', axis=1, tiled=True)  74 us
    reduce_scatter x1, waiting for transfers between devices, local(): lax.psum_scatter(lax.dot_general(back_rot, basis_cols, contract_last, pre...  50 us
    all_gather x1, waiting for transfers between devices, local(): basis_block = lax.all_gather(eigvecs, 'rows', axis=1, tiled=True)  32.3 us
    all_gather x1, waiting for transfers between devices, local(): sens_scaled = lax.all_gather(scaled_own, 'rows', axis=0, tiled=True)  27.9 us
    psum x1, blocking collectives, local(): lax.psum((cross_one, cross_two, sum_x, sum_g), 'rows')  25.6 us
  transfers between devices with their start and end apart: 8, of which 8 were waited for; matrix products, arithmetic and copies ran while one was open for 5% of the time, Pallas kernels for 0%

commit v1 on v0

--- a/solution.py
+++ b/solution.py
@@ -67,7 +67,7 @@
     )
     scaled_own = (2.0 / row_count * sens_own).astype(jnp.bfloat16)
     sens_scaled = lax.all_gather(scaled_own, "rows", axis=0, tiled=True)
-    piece_x = lax.all_gather(features, "feat", axis=1, tiled=True)
+    piece_x = jnp.concatenate(lax.all_gather(features, "feat"), 1)
     piece_g = lax.all_gather(grad_out, "feat", axis=1, tiled=True)
     shifted = (piece_g.astype(jnp.float32) - grad_mean).astype(jnp.bfloat16)
     centered = (piece_x.astype(jnp.float32) - col_mean).astype(jnp.bfloat16)

time: 552 us -> 627 us (1.14)
  waiting for transfers between devices: 447 us -> 506 us
  other arithmetic: 5.43 us -> 17.9 us
  local copies, waits for them, and re-layouts: 0.75 us -> 9.52 us
  matrix products: 59.6 us -> 53.3 us
    all_gather x0 -> x1, waiting for transfers between devices: none -> 80.6 us  [local(): piece_x = jnp.concatenate(lax.all_gather(features, 'feat'), 1)]
    all_gather x1, waiting for transfers between devices: 27.9 us -> 6.96 us  [local(): sens_scaled = lax.all_gather(scaled_own, 'rows', axis=0, tiled=True)]
    convert_element_type x0 -> x2, other arithmetic: none -> 12.5 us  [local(): centered = (piece_x.astype(jnp.float32) - col_mean).astype(jnp.bfloat16)]
    convert_element_type x0 -> x1, local copies, waits for them, and re-layouts: none -> 8.77 us  [local(): centered = (piece_x.astype(jnp.float32) - col_mean).astype(jnp.bfloat16)]
  transfers between devices with their start and end apart: 8 -> 9, of which waited for: 8 -> 9; matrix products, arithmetic and copies ran while one was open for 5% -> 8% of each run, Pallas kernels for 0% -> 0%
where the time goes in v1:
time: 627 us
  waiting for transfers between devices  506 us (81%)
  matrix products  53.3 us (9%)
  blocking collectives  25.6 us (4%)
  other arithmetic  17.9 us (3%)
  between operations  13.3 us (2%)
  local copies, waits for them, and re-layouts  9.52 us (2%)
    psum x1, waiting for transfers between devices, local(): rotated = lax.psum(partial_value, 'feat')  85.9 us
    all_gather x1, waiting for transfers between devices, local(): piece_g = lax.all_gather(grad_out, 'feat', axis=1, tiled=True)  83.6 us
    psum x1, waiting for transfers between devices, local(): lax.psum((cross_one, cross_two, sum_x, sum_g), 'rows')  82.8 us
    all_gather x1, waiting for transfers between devices, local(): piece_x = jnp.concatenate(lax.all_gather(features, 'feat'), 1)  80.6 us
    all_gather x1, waiting for transfers between devices, local(): piece_x = lax.all_gather(features, 'feat', axis=1, tiled=True)  74 us
    reduce_scatter x1, waiting for transfers between devices, local(): lax.psum_scatter(lax.dot_general(back_rot, basis_cols, contract_last, pre...  49.5 us
    all_gather x1, waiting for transfers between devices, local(): basis_block = lax.all_gather(eigvecs, 'rows', axis=1, tiled=True)  32.3 us
    psum x1, blocking collectives, local(): lax.psum((cross_one, cross_two, sum_x, sum_g), 'rows')  25.6 us
  transfers between devices with their start and end apart: 9, of which 9 were waited for; matrix products, arithmetic and copies ran while one was open for 8% of the time, Pallas kernels for 0%

profile of v1, /device:TPU:0, one launch (start us, length us, event | category | flops | bytes accessed | tf_op | source)
XLA Modules:
  0.0 626.6 jit_solution(15199631131642859101)
XLA Ops:
  6.5 0.7 all-gather.8.cloned.1.call-update
  7.3 0.7 all-gather.10.cloned.1.call-update
  8.1 0.7 all-gather.12.cloned.1.call-update
  8.8 83.6 %all-gather.8.cloned.1.call-done = bf16[1024,2048]{1,0:T(8,128)(2,1)} async-done(((bf16[1024,512]{1,0:T(8,128)(2,1)}), bf16[1024,2048]{1,0:T(8,128)(2,1)}) %all-gather.8.cloned.1.call-update) | async-done | bytes 4194320 | tf_op jit(solution)/shard_map/all_gather | solution.py:71
  92.4 6.8 %fusion.37 = f32[512,2048]{1,0:T(8,128)} fusion(bf16[1024,512]{1,0:T(8,128)(2,1)} %param.5, bf16[1024,2048]{1,0:T(8,128)(2,1)} %all-gather.8.cloned.1.call-done), kind=kOutput, calls=%fused_computation.50 | convolution fusion | flops 2147483648 | bytes 9437184 | tf_op jit(solution)/shard_map/dot_general | solution.py:29
  99.2 74.0 %all-gather.10.cloned.1.call-done = bf16[1024,2048]{1,0:T(8,128)(2,1)} async-done(((bf16[1024,512]{1,0:T(8,128)(2,1)}), bf16[1024,2048]{1,0:T(8,128)(2,1)}) %all-gather.10.cloned.1.call-update) | async-done | bytes 4194320 | tf_op jit(solution)/shard_map/all_gather | solution.py:27
  173.2 7.8 %convolution_add_fusion = f32[512,2048]{1,0:T(8,128)} fusion(f32[512,2048]{1,0:T(8,128)} %fusion.37, bf16[1024,512]{1,0:T(8,128)(2,1)S(1)} %copy-done.3, bf16[1024,2048]{1,0:T(8,128)(2,1)} %all-gather.10.cloned.1.call-done), kind=kOutput, calls=%fused_computation.16 | convolution fusion | flops 2148532224 | bytes 13631488 | tf_op jit(solution)/shard_map/dot_general | solution.py:32
  181.1 0.5 all-gather.14.cloned.1.call-update
  181.7 3.0 convert_reduce_fusion
  184.7 0.5 copy-done.2
  185.2 0.6 convert_reduce_fusion.1
  185.8 25.6 %all-reduce = (f32[2048]{0:T(1024)S(1)}, f32[2048]{0:T(1024)S(1)}) all-reduce(f32[2048]{0:T(1024)S(1)} %convert_reduce_fusion.1, f32[2048]{0:T(1024)S(1)} %convert_reduce_fusion), channel_id=1, replica_groups=mesh['rows'=8,'feat'=4] {'rows'}, use_global_device_ids=true, to_apply=%region_3.0 | all-reduce | flops 4096 | bytes 32768 | tf_op jit(solution)/shard_map/psum | solution.py:40
  211.5 7.4 %all-gather.12.cloned.1.call-done = f32[2048,256]{1,0:T(8,128)} async-done(((f32[512,256]{1,0:T(8,128)}), f32[2048,256]{1,0:T(8,128)}) %all-gather.12.cloned.1.call-update) | async-done | bytes 2097168 | tf_op jit(solution)/shard_map/all_gather | solution.py:52
  219.0 82.8 %all-reduce.6.cloned.1.call-done = f32[512,2048]{1,0:T(8,128)} async-done(((f32[512,2048]{1,0:T(8,128)}), f32[512,2048]{1,0:T(8,128)}) %all-reduce.6.cloned.1.call-update) | async-done | bytes 4194320 | tf_op jit(solution)/shard_map/psum | solution.py:40
  301.7 6.9 %fusion.4 = f32[512,256]{1,0:T(8,128)S(1)} fusion(f32[2048,256]{1,0:T(8,128)} %all-gather.12.cloned.1.call-done, f32[512,2048]{1,0:T(8,128)} %all-reduce.6.cloned.1.call-done, f32[2048]{0:T(1024)S(1)} %get-tuple-element.11, f32[512]{0:T(512)S(1)} %dynamic_slice.11, f32[2048]{0:T(1024)S(1)} %get-tuple-element.12, f32[512]{0:T(512)S(1)} %dynamic_slice.10), kind=kOutput, calls=%fused_computation.8 | convolution fusion | flops 3227516928 | bytes 6836224 | tf_op jit(solution)/shard_map/dot_general | solution.py:55
  308.6 32.3 %all-gather.14.cloned.1.call-done = f32[512,2048]{1,0:T(8,128)} async-done(((f32[512,256]{1,0:T(8,128)}), f32[512,2048]{1,0:T(8,128)}) %all-gather.14.cloned.1.call-update) | async-done | bytes 4194320 | tf_op jit(solution)/shard_map/all_gather | solution.py:53
  340.9 7.1 %convolution_bitcast_fusion = f32[2048,256]{0,1:T(8,128)} fusion(f32[512,256]{1,0:T(8,128)S(1)} %fusion.4, f32[512,2048]{1,0:T(8,128)} %all-gather.14.cloned.1.call-done), kind=kOutput, calls=%fused_computation.17 | convolution fusion | flops 3221225472 | bytes 6815744 | tf_op jit(solution)/shard_map/dot_general | solution.py:56
  348.1 0.3 reduce-scatter.2.cloned.1.call-start
  348.4 0.1 broadcast_power_fusion.1
  348.5 85.9 %all-reduce.4.cloned.1.call-done = f32[2048,256]{0,1:T(8,128)} async-done(((f32[2048,256]{0,1:T(8,128)}), f32[2048,256]{0,1:T(8,128)}) %all-reduce.4.cloned.1.call-update) | async-done | bytes 2097168 | tf_op jit(solution)/shard_map/psum | solution.py:57
  434.4 7.6 %fusion.12 = f32[256,512]{1,0:T(8,128)S(1)} fusion(f32[512,2048]{1,0:T(8,128)} %all-gather.14.cloned.1.call-done, f32[2048,256]{0,1:T(8,128)} %all-reduce.4.cloned.1.call-done, f32[256]{0:T(256)S(1)} %get-tuple-element.8, f32[2048]{0:T(1024)S(1)} %copy-done.5, f32[256]{0:T(256)S(1)} %get-tuple-element.7, f32[2048]{0:T(1024)S(1)} %get-tuple-element.10, ...), kind=kOutput, calls=%fused_computation.19 | convolution fusion | flops 3224895488 | bytes 6843392 | tf_op jit(solution)/shard_map/dot_general | solution.py:61
  442.0 8.5 %fusion.38 = f32[512,2048]{1,0:T(8,128)} fusion(f32[256,512]{1,0:T(8,128)S(1)} %fusion.12, f32[2048,256]{1,0:T(8,128)S(1)} %copy-done.4), kind=kOutput, calls=%fused_computation.51 | convolution fusion | flops 3221225472 | bytes 6815744 | tf_op jit(solution)/shard_map/dot_general | solution.py:63
  450.5 0.7 all-gather.18.cloned.1.call-update
  451.3 49.5 %reduce-scatter.2.cloned.1.call-done = f32[64,2048]{1,0:T(8,128)} async-done(((f32[512,2048]{1,0:T(8,128)}), f32[64,2048]{1,0:T(8,128)}) %reduce-scatter.2.cloned.1.call-update) | async-done | bytes 524304 | tf_op jit(solution)/shard_map/reduce_scatter | solution.py:62
  500.8 1.8 multiply_convert_fusion
  502.6 80.6 %all-gather.18.cloned.1.call-done = bf16[4096,512]{1,0:T(8,128)(2,1)} async-done(((bf16[1024,512]{1,0:T(8,128)(2,1)}), bf16[4096,512]{1,0:T(8,128)(2,1)}) %all-gather.18.cloned.1.call-update) | async-done | bytes 4194320 | tf_op jit(solution)/shard_map/all_gather | solution.py:70
  583.2 6.6 %convert_bitcast_fusion = f32[1024,4,512]{2,0,1:T(8,128)} fusion(bf16[4,1024,512]{2,1,0:T(8,128)(2,1)} %bitcast.23), kind=kLoop, calls=%fused_computation.3 | loop fusion | flops 2097152 | bytes 12582912 | tf_op jit(solution)/shard_map/convert_element_type | solution.py:73
  589.8 8.8 %copy.6 = f32[1024,4,512]{0,2,1:T(8,128)} copy(f32[1024,4,512]{2,0,1:T(8,128)} %convert_bitcast_fusion) | data formatting | bytes 16777216 | tf_op jit(solution)/shard_map/convert_element_type | solution.py:73
  598.6 5.8 fusion.1
  604.4 7.0 %all-gather.16.cloned.1.call-done = bf16[512,2048]{1,0:T(8,128)(2,1)} async-done(((bf16[64,2048]{1,0:T(8,128)(2,1)}), bf16[512,2048]{1,0:T(8,128)(2,1)}) %all-gather.16.cloned.1.call-update) | async-done | bytes 2097168 | tf_op jit(solution)/shard_map/all_gather | solution.py:69
  611.4 5.4 fusion.39
  616.8 3.3 add_convert_fusion
  (28 shorter events, 0.5 us)
Async XLA Ops:
  6.5 610.2 %copy-start = (bf16[2048,512]{1,0:T(8,128)(2,1)S(1)}, bf16[2048,512]{1,0:T(8,128)(2,1)}, u32[]{:S(2)}) copy-start(bf16[2048,512]{1,0:T(8,128)(2,1)} %param.9) | copy-start | bytes 6291460
  6.5 85.9 %all-gather.8.cloned.1.call-start = ((), (), s32[]{:S(2)}) async-start(), calls=%async_computation.1 | async-start | bytes 5242880 | tf_op jit(solution)/shard_map/all_gather | solution.py:71
  7.3 166.0 %all-gather.10.cloned.1.call-start = ((), (), s32[]{:S(2)}) async-start(), calls=%async_computation.2 | async-start | bytes 5242880 | tf_op jit(solution)/shard_map/all_gather | solution.py:27
  8.0 211.0 %all-gather.12.cloned.1.call-start = ((), (), s32[]{:S(2)}) async-start(), calls=%async_computation.3 | async-start | bytes 2621440 | tf_op jit(solution)/shard_map/all_gather | solution.py:52
  8.7 164.5 %copy-start.3 = (bf16[1024,512]{1,0:T(8,128)(2,1)S(1)}, bf16[1024,512]{1,0:T(8,128)(2,1)}, u32[]{:S(2)}) copy-start(bf16[1024,512]{1,0:T(8,128)(2,1)} %param.6) | copy-start | bytes 3145732
  8.8 293.0 %all-reduce.6.cloned.1.call-start = ((), (), s32[]{:S(2)}) async-start(), calls=%async_computation.9 | async-start | bytes 8388608 | tf_op jit(solution)/shard_map/psum | solution.py:40
  181.0 159.9 %all-gather.14.cloned.1.call-start = ((), (), s32[]{:S(2)}) async-start(), calls=%async_computation.4 | async-start | bytes 4718592 | tf_op jit(solution)/shard_map/all_gather | solution.py:53
  181.6 252.8 %all-reduce.4.cloned.1.call-start = ((), (), s32[]{:S(2)}) async-start(), calls=%async_computation.5 | async-start | bytes 4194304 | tf_op jit(solution)/shard_map/psum | solution.py:57
  181.7 3.5 copy-start.2
  308.6 39.7 %copy-start.5 = (f32[2048]{0:T(1024)S(1)}, f32[2048]{0:T(1024)}, u32[]{:S(2)}) copy-start(f32[2048]{0:T(1024)} %param.8) | copy-start | bytes 24580
  348.1 152.7 %reduce-scatter.2.cloned.1.call-start = ((), (), s32[]{:S(2)}) async-start(), calls=%async_computation.6 | async-start | bytes 4718592 | tf_op jit(solution)/shard_map/reduce_scatter | solution.py:62
  434.4 7.6 %copy-start.4 = (f32[2048,256]{1,0:T(8,128)S(1)}, f32[2048,256]{1,0:T(8,128)}, u32[]{:S(2)}) copy-start(f32[2048,256]{1,0:T(8,128)} %all-gather.12.cloned.1.call-done) | copy-start | bytes 6291460
  450.5 132.7 %all-gather.18.cloned.1.call-start = ((), (), s32[]{:S(2)}) async-start(), calls=%async_computation.8 | async-start | bytes 5242880 | tf_op jit(solution)/shard_map/all_gather | solution.py:70
  451.2 160.1 %all-gather.16.cloned.1.call-start = ((), (), s32[]{:S(2)}) async-start(), calls=%async_computation.7 | async-start | bytes 2359296 | tf_op jit(solution)/shard_map/all_gather | solution.py:69
  611.4 5.4 copy-start.1
Sparse Core Ops, SparseCore 0:
  8.9 83.4 all-gather.7
  94.0 79.2 all-gather.9
  174.8 44.1 all-gather.11
  222.1 79.5 all-reduce.5
  303.5 37.3 all-gather.13
  348.2 86.1 all-reduce.3
  450.6 50.1 reduce-scatter.1
  502.4 80.7 all-gather.17
  585.1 26.2 all-gather.15
